TPU v7x, 256 devices: a whole 4x4x8 slice. The times are simulated.
256 devices in a mesh: seq: 128 (over y, z, x_hi, core), batch: 2 (over x_lo).
Axes of the slice: x: 4 (x_hi: 2, x_lo: 2; x = x_hi * 2 + x_lo), y: 4, z: 8, core: 2. Of those that a mesh axis runs over, the one named last changes fastest.
Arguments:
- stream_in: bfloat16 [320, 2097152], P(None, ('batch', 'seq')), parts along dimension 1, may hold values from -6 to 6
- norm_gains: float32 [2, 320], replicated, may hold values from 0.5 to 1.5
- w_inner: bfloat16 [2, 320, 640], replicated, may hold values from -0.3125 to 0.3125
- w_outer: bfloat16 [2, 640, 320], replicated, may hold values from -0.25 to 0.25
Outputs:
- stream_out: bfloat16 [320, 2097152], P(None, ('batch', 'seq')), parts along dimension 1
There are 2 independent parts, one for each index of `batch`. A program takes and returns all parts, laid end to end along the dimension named above; an argument that names none is the same for every part. Nothing has to cross between parts.
All inputs are finite; a program needn't handle non-finite values.
Results may differ from a plain program's by a relative error of at most 0.0059.
Values may be sent and summed in bfloat16 or wider, within the bound.
A program may use at most 64 MiB of HBM per device.

v0:
```python
import functools

import jax
import jax.numpy as jnp
from jax import lax
from jax.experimental import pallas as pl
from jax.experimental.pallas import tpu as pltpu
from jax.sharding import PartitionSpec as P

TRACKS = 20
WIDTH = 16
LAYERS = 2
DIM = 320
HID = 640
RING = 128
COLS = 8192
NEAR = 13
NEAR_ROWS = NEAR * WIDTH
FAR_ROWS = DIM - NEAR_ROWS
PAD = 4096
CHUNKS = 8
CHUNK = COLS // CHUNKS
SUB = 256
LANES = 128
FAR = tuple(2**e for e in range(TRACKS - NEAR))

HALOS = (
    (0, 128, 128, 7),
    (128, 16, 256, 7),
    (144, 16, 512, 7),
    (192, 16, 1024, 4),
    (192, 16, 1024, 5),
    (176, 32, 1024, 6),
    (160, 48, 1024, 7),
)


def halo_slices(index):
    row, rows, cols, chunk = HALOS[index]
    start = (chunk + 1) * CHUNK - cols
    return pl.ds(row, rows), start, cols


def body(
    x_ref, gain_ref, inner_ref, outer_ref, out_ref,
    near, far, made, gains, inner_t, outer_t, inner_raw, outer_raw, rotated, staged,
    local_sem, weight_sem, far_send, far_recv, halo_send, halo_recv, out_sem,
):
    me = lax.axis_index("seq")
    ahead = [lax.rem(me + d, RING) for d in FAR]
    behind = [lax.rem(me + RING - d, RING) for d in FAR]

    near_copy = pltpu.make_async_copy(
        x_ref.at[pl.ds(0, NEAR_ROWS), :], near.at[0, :, pl.ds(PAD, COLS)], local_sem
    )
    near_copy.start()
    inner_copy = pltpu.make_async_copy(inner_ref, inner_raw, weight_sem.at[0])
    outer_copy = pltpu.make_async_copy(outer_ref, outer_raw, weight_sem.at[1])
    inner_copy.start()
    outer_copy.start()

    barrier = pltpu.get_barrier_semaphore()
    for peer in ahead + behind:
        pl.semaphore_signal(barrier, inc=1, device_id={"seq": peer})
    pl.semaphore_wait(barrier, 2 * len(FAR))

    def halo_copy(layer, index, source):
        rows, start, cols = halo_slices(index)
        return pltpu.make_async_remote_copy(
            src_ref=source.at[rows, pl.ds(start + (0 if layer == 0 else PAD), cols)],
            dst_ref=near.at[layer, rows, pl.ds(start + PAD - COLS, cols)],
            send_sem=halo_send.at[layer, index],
            recv_sem=halo_recv.at[layer, index],
            device_id={"seq": ahead[0]},
        )

    def far_copy(layer, track, chunk, source, base):
        cols = pl.ds(pl.multiple_of(chunk * CHUNK, CHUNK), CHUNK)
        return pltpu.make_async_remote_copy(
            src_ref=source.at[pl.ds(base + track * WIDTH, WIDTH), cols],
            dst_ref=far.at[layer, pl.ds(track * WIDTH, WIDTH), cols],
            send_sem=far_send.at[layer],
            recv_sem=far_recv.at[layer, chunk],
            device_id={"seq": ahead[track]},
        )

    def send_far(layer, chunk, source, base):
        for track in range(len(FAR)):
            far_copy(layer, track, chunk, source, base).start()

    for index in range(len(HALOS)):
        halo_copy(0, index, x_ref).start()

    @pl.loop(0, CHUNKS)
    def _(step):
        send_far(0, lax.rem(step + CHUNKS // 2, CHUNKS), x_ref, NEAR_ROWS)

    for layer in range(LAYERS):
        gains[layer] = jnp.broadcast_to(gain_ref[layer : layer + 1, :], (LANES, DIM)).T
    inner_copy.wait()
    for layer in range(LAYERS):
        inner_t[layer] = inner_raw[layer].T
    outer_copy.wait()
    for layer in range(LAYERS):
        outer_t[layer] = outer_raw[layer].T
    near_copy.wait()

    def mix(layer, at, store):
        base = pl.multiple_of(PAD + at, LANES)
        for track in range(NEAR):
            shift = 2**track
            rows = pl.ds(track * WIDTH, WIDTH)
            if shift < LANES:
                wide = near[layer, rows, pl.ds(pl.multiple_of(base - LANES, LANES), SUB + LANES)]
                piece = pltpu.roll(wide.astype(jnp.float32), shift, 1)[:, LANES:]
            else:
                piece = near[layer, rows, pl.ds(pl.multiple_of(base - shift, LANES), SUB)].astype(jnp.float32)
            rotated[rows, :] = piece
        rotated[NEAR_ROWS:, :] = far[layer, :, pl.ds(pl.multiple_of(at, LANES), SUB)].astype(jnp.float32)
        values = rotated[...]
        average = jnp.sum(values, axis=0, keepdims=True) * (1.0 / DIM)
        centred = values - average
        spread = jnp.sum(centred * centred, axis=0, keepdims=True) * (1.0 / DIM)
        scale = lax.rsqrt(spread + 1e-05)
        gain = jnp.concatenate([gains[layer]] * (SUB // LANES), axis=1)
        normed = (centred * scale * gain).astype(jnp.bfloat16)
        inner_sum = jnp.dot(inner_t[layer], normed, preferred_element_type=jnp.float32)
        hidden = (0.5 * inner_sum * (1.0 + lax.erf(inner_sum * (0.5**0.5)))).astype(jnp.bfloat16)
        outer_sum = jnp.dot(outer_t[layer], hidden, preferred_element_type=jnp.float32)
        store((rotated[...] + outer_sum).astype(jnp.bfloat16))

    def wait_far(layer, chunk):
        cols = pl.ds(pl.multiple_of(chunk * CHUNK, CHUNK), CHUNK)
        whole = far.at[layer, :, cols]
        pltpu.make_async_copy(whole, whole, far_recv.at[layer, chunk]).wait()

    def wait_halos(layer, source):
        for index in range(len(HALOS)):
            halo_copy(layer, index, source).wait_recv()

    @pl.loop(0, CHUNKS)
    def _(step):
        chunk = lax.rem(step + CHUNKS // 2, CHUNKS)
        wait_far(0, chunk)

        @pl.when(step == CHUNKS // 2)
        def _():
            wait_halos(0, x_ref)

        @pl.loop(0, CHUNK // SUB)
        def _(part):
            at = pl.multiple_of(chunk * CHUNK + part * SUB, SUB)

            def store(result):
                near[1, :, pl.ds(pl.multiple_of(PAD + at, SUB), SUB)] = result[:NEAR_ROWS]
                made[:, pl.ds(at, SUB)] = result[NEAR_ROWS:]

            mix(0, at, store)

        send_far(1, chunk, made, 0)
        for index, halo in enumerate(HALOS):
            @pl.when(chunk == halo[3])
            def _():
                halo_copy(1, index, near.at[1]).start()

    def out_copy(slot, chunk):
        cols = pl.ds(pl.multiple_of(chunk * CHUNK, CHUNK), CHUNK)
        return pltpu.make_async_copy(staged.at[slot], out_ref.at[:, cols], out_sem.at[slot])

    @pl.loop(0, CHUNKS)
    def _(step):
        chunk = lax.rem(step + CHUNKS // 2, CHUNKS)
        slot = lax.rem(step, 2)
        wait_far(1, chunk)

        @pl.when(step == CHUNKS // 2)
        def _():
            wait_halos(1, near.at[1])

        @pl.when(step >= 2)
        def _():
            out_copy(slot, chunk).wait()

        @pl.loop(0, CHUNK // SUB)
        def _(part):
            at = pl.multiple_of(chunk * CHUNK + part * SUB, SUB)

            def store(result):
                staged[slot, :, pl.ds(pl.multiple_of(part * SUB, SUB), SUB)] = result

            mix(1, at, store)

        out_copy(slot, chunk).start()

    out_copy(0, 0).wait()
    out_copy(1, 0).wait()
    for layer in range(LAYERS):
        source = x_ref if layer == 0 else near.at[1]
        for index in range(len(HALOS)):
            halo_copy(layer, index, source).wait_send()
        pltpu.make_async_copy(far.at[layer], far.at[layer], far_send.at[layer]).wait()


def per_device(stream_in, norm_gains, w_inner, w_outer):
    hbm = pl.BlockSpec(memory_space=pl.ANY)
    return pl.pallas_call(
        body,
        out_shape=jax.ShapeDtypeStruct(stream_in.shape, stream_in.dtype),
        in_specs=[hbm, pl.BlockSpec(memory_space=pltpu.VMEM), hbm, hbm],
        out_specs=hbm,
        scratch_shapes=[
            pltpu.VMEM((LAYERS, NEAR_ROWS, PAD + COLS), jnp.bfloat16),
            pltpu.VMEM((LAYERS, FAR_ROWS, COLS), jnp.bfloat16),
            pltpu.VMEM((FAR_ROWS, COLS), jnp.bfloat16),
            pltpu.VMEM((LAYERS, DIM, LANES), jnp.float32),
            pltpu.VMEM((LAYERS, HID, DIM), jnp.bfloat16),
            pltpu.VMEM((LAYERS, DIM, HID), jnp.bfloat16),
            pltpu.VMEM((LAYERS, DIM, HID), jnp.bfloat16),
            pltpu.VMEM((LAYERS, HID, DIM), jnp.bfloat16),
            pltpu.VMEM((DIM, SUB), jnp.float32),
            pltpu.VMEM((2, DIM, CHUNK), jnp.bfloat16),
            pltpu.SemaphoreType.DMA,
            pltpu.SemaphoreType.DMA((2,)),
            pltpu.SemaphoreType.DMA((LAYERS,)),
            pltpu.SemaphoreType.DMA((LAYERS, CHUNKS)),
            pltpu.SemaphoreType.DMA((LAYERS, len(HALOS))),
            pltpu.SemaphoreType.DMA((LAYERS, len(HALOS))),
            pltpu.SemaphoreType.DMA((2,)),
        ],
        compiler_params=pltpu.CompilerParams(
            collective_id=0, has_side_effects=True, vmem_limit_bytes=60 * 1024 * 1024
        ),
    )(stream_in, norm_gains, w_inner, w_outer)


def solution(mesh):
    return jax.shard_map(
        per_device,
        mesh=mesh,
        in_specs=(P(None, ("batch", "seq")), P(), P(), P()),
        out_specs=P(None, ("batch", "seq")),
        check_vma=False,
    )
```

profile of v0, /device:TPU:2, one launch (start us, length us, event | category | flops | bytes accessed | tf_op | source)
XLA Modules:
  0.0 125.8 jit_solution(10261151701005415230)
XLA Ops:
  0.0 2.2 %copy.5.outer_ref = bf16[2,640,320]{2,1,0:T(8,128)(2,1)} copy(bf16[2,640,320]{1,2,0:T(8,128)(2,1)} %param.7) | data formatting | bytes 1638400 | tf_op args[3]
  2.2 118.2 %shard_map.46 = bf16[320,8192]{1,0:T(8,128)(2,1)} custom-call(bf16[320,8192]{1,0:T(8,128)(2,1)} %x_ref.1, f32[2,320]{1,0:T(2,128)} %gain_ref.1, bf16[2,320,640]{2,1,0:T(8,128)(2,1)} %inner_ref.1, bf16[2,640,320]{2,1,0:T(8,128)(2,1)} %copy.5.outer_ref), custom_call_target="tpu_custom_call" | custom-call | tf_op jit(solution)/shard_map/pallas_call | solution.py:206
  120.4 5.4 %copy.7 = bf16[320,8192]{1,0:T(8,128)(2,1)} copy(bf16[320,8192]{1,0:T(8,128)(2,1)} %shard_map.46) | data formatting | bytes 10485760
where the time goes:
time: 126 us
  Pallas kernels  118 us (94%)
  local copies, waits for them, and re-layouts  7.64 us (6%)
    pallas_call x1, Pallas kernels, per_device(): pl.pallas_call(body, out_shape=jax.ShapeDtypeStruct(stream_in.shape, stre...  118 us
    unnamed x2, local copies, waits for them, and re-layouts  7.64 us

commit v1 on v0

--- a/solution.py
+++ b/solution.py
@@ -20,9 +20,12 @@
 PAD = 4096
 CHUNKS = 8
 CHUNK = COLS // CHUNKS
-SUB = 256
+SUB = 512
 LANES = 128
 FAR = tuple(2**e for e in range(TRACKS - NEAR))
+HOP2, HOP8, HOP16 = range(3)
+HOP_TRACK = (1, 3, 4)
+LEAD = 2
 
 HALOS = (
     (0, 128, 128, 7),
@@ -43,26 +46,55 @@
 
 def body(
     x_ref, gain_ref, inner_ref, outer_ref, out_ref,
-    near, far, made, gains, inner_t, outer_t, inner_raw, outer_raw, rotated, staged,
-    local_sem, weight_sem, far_send, far_recv, halo_send, halo_recv, out_sem,
+    near, far, made, hop, gains, inner_t, inner_raw, outer_t, rotated, staged,
+    local_sem, weight_sem, far_send, far_recv, hop_send, hop_recv, halo_send, halo_recv, out_sem,
 ):
     me = lax.axis_index("seq")
+    row, depth = me // 32, lax.rem(me // 4, 8)
+    half, core = lax.rem(me // 2, 2), lax.rem(me, 2)
+
+    def device(y, z, x):
+        return ((lax.rem(y + 4, 4) * 8 + lax.rem(z + 8, 8)) * 2 + x) * 2 + core
+
     ahead = [lax.rem(me + d, RING) for d in FAR]
     behind = [lax.rem(me + RING - d, RING) for d in FAR]
+    deep = jnp.where(depth >= 4, 1, 0)
+    last = jnp.where(depth == 7, 1, 0)
+    hop_to = [
+        device(row + last * half, depth, 1 - half),
+        device(row + 1, depth, half),
+        device(row + deep, depth - 2, half),
+    ]
+    hop_from = [
+        device(row - last * (1 - half), depth, 1 - half),
+        device(row - 1, depth, half),
+        device(row - jnp.where(lax.rem(depth + 2, 8) >= 4, 1, 0), depth + 2, half),
+    ]
+    pass_to = [device(row, depth + 1, half), device(row, depth + 2, half), device(row, depth - 2, half)]
+    pass_from = [device(row, depth - 1, half), device(row, depth - 2, half), device(row, depth + 2, half)]
+    sends_hop = [half == 1, depth == 6, None]
+    passes = [half == 0, depth == 6, None]
+
+    def where(condition, action):
+        if condition is None:
+            action()
+        else:
+            pl.when(condition)(action)
 
     near_copy = pltpu.make_async_copy(
         x_ref.at[pl.ds(0, NEAR_ROWS), :], near.at[0, :, pl.ds(PAD, COLS)], local_sem
     )
     near_copy.start()
     inner_copy = pltpu.make_async_copy(inner_ref, inner_raw, weight_sem.at[0])
-    outer_copy = pltpu.make_async_copy(outer_ref, outer_raw, weight_sem.at[1])
+    outer_copy = pltpu.make_async_copy(outer_ref, outer_t, weight_sem.at[1])
     inner_copy.start()
     outer_copy.start()
 
     barrier = pltpu.get_barrier_semaphore()
-    for peer in ahead + behind:
+    peers = ahead + behind + hop_to + hop_from + pass_to + pass_from
+    for peer in peers:
         pl.semaphore_signal(barrier, inc=1, device_id={"seq": peer})
-    pl.semaphore_wait(barrier, 2 * len(FAR))
+    pl.semaphore_wait(barrier, len(peers))
 
     def halo_copy(layer, index, source):
         rows, start, cols = halo_slices(index)
@@ -84,9 +116,45 @@
             device_id={"seq": ahead[track]},
         )
 
+    def hop_copy(layer, kind, chunk, source, base):
+        cols = pl.ds(pl.multiple_of(chunk * CHUNK, CHUNK), CHUNK)
+        return pltpu.make_async_remote_copy(
+            src_ref=source.at[pl.ds(base + HOP_TRACK[kind] * WIDTH, WIDTH), cols],
+            dst_ref=hop.at[layer, kind, :, cols],
+            send_sem=far_send.at[layer],
+            recv_sem=hop_recv.at[layer, kind, chunk],
+            device_id={"seq": hop_to[kind]},
+        )
+
+    def pass_copy(layer, kind, chunk):
+        cols = pl.ds(pl.multiple_of(chunk * CHUNK, CHUNK), CHUNK)
+        return pltpu.make_async_remote_copy(
+            src_ref=hop.at[layer, kind, :, cols],
+            dst_ref=far.at[layer, pl.ds(HOP_TRACK[kind] * WIDTH, WIDTH), cols],
+            send_sem=hop_send.at[layer, kind],
+            recv_sem=far_recv.at[layer, chunk],
+            device_id={"seq": pass_to[kind]},
+        )
+
     def send_far(layer, chunk, source, base):
+        for kind in (HOP16, HOP8, HOP2):
+            where(sends_hop[kind], lambda: hop_copy(layer, kind, chunk, source, base).start())
         for track in range(len(FAR)):
-            far_copy(layer, track, chunk, source, base).start()
+            kind = HOP_TRACK.index(track) if track in HOP_TRACK else None
+            if kind == HOP16:
+                continue
+            direct = None if kind is None else jnp.logical_not(sends_hop[kind])
+            where(direct, lambda: far_copy(layer, track, chunk, source, base).start())
+
+    def forward(layer, chunk):
+        cols = pl.ds(pl.multiple_of(chunk * CHUNK, CHUNK), CHUNK)
+        for kind in (HOP16, HOP8, HOP2):
+            def relay():
+                landed = hop.at[layer, kind, :, cols]
+                pltpu.make_async_copy(landed, landed, hop_recv.at[layer, kind, chunk]).wait()
+                pass_copy(layer, kind, chunk).start()
+
+            where(passes[kind], relay)
 
     for index in range(len(HALOS)):
         halo_copy(0, index, x_ref).start()
@@ -101,8 +169,6 @@
     for layer in range(LAYERS):
         inner_t[layer] = inner_raw[layer].T
     outer_copy.wait()
-    for layer in range(LAYERS):
-        outer_t[layer] = outer_raw[layer].T
     near_copy.wait()
 
     def mix(layer, at, store):
@@ -138,9 +204,24 @@
         for index in range(len(HALOS)):
             halo_copy(layer, index, source).wait_recv()
 
+    def turn(step):
+        return lax.rem(step + CHUNKS // 2, CHUNKS)
+
+    for step in range(LEAD):
+        forward(0, turn(step))
+
     @pl.loop(0, CHUNKS)
     def _(step):
-        chunk = lax.rem(step + CHUNKS // 2, CHUNKS)
+        chunk = turn(step)
+
+        @pl.when(step < CHUNKS - LEAD)
+        def _():
+            forward(0, turn(step + LEAD))
+
+        @pl.when(step >= CHUNKS // 2)
+        def _():
+            forward(1, turn(step - CHUNKS // 2))
+
         wait_far(0, chunk)
 
         @pl.when(step == CHUNKS // 2)
@@ -171,6 +252,11 @@
     def _(step):
         chunk = lax.rem(step + CHUNKS // 2, CHUNKS)
         slot = lax.rem(step, 2)
+
+        @pl.when(step < CHUNKS // 2)
+        def _():
+            forward(1, turn(step + CHUNKS // 2))
+
         wait_far(1, chunk)
 
         @pl.when(step == CHUNKS // 2)
@@ -199,6 +285,9 @@
         for index in range(len(HALOS)):
             halo_copy(layer, index, source).wait_send()
         pltpu.make_async_copy(far.at[layer], far.at[layer], far_send.at[layer]).wait()
+        for kind in (HOP16, HOP8, HOP2):
+            kept = hop.at[layer, kind]
+            where(passes[kind], lambda: pltpu.make_async_copy(kept, kept, hop_send.at[layer, kind]).wait())
 
 
 def per_device(stream_in, norm_gains, w_inner, w_outer):
@@ -212,17 +301,19 @@
             pltpu.VMEM((LAYERS, NEAR_ROWS, PAD + COLS), jnp.bfloat16),
             pltpu.VMEM((LAYERS, FAR_ROWS, COLS), jnp.bfloat16),
             pltpu.VMEM((FAR_ROWS, COLS), jnp.bfloat16),
+            pltpu.VMEM((LAYERS, 3, WIDTH, COLS), jnp.bfloat16),
             pltpu.VMEM((LAYERS, DIM, LANES), jnp.float32),
             pltpu.VMEM((LAYERS, HID, DIM), jnp.bfloat16),
             pltpu.VMEM((LAYERS, DIM, HID), jnp.bfloat16),
             pltpu.VMEM((LAYERS, DIM, HID), jnp.bfloat16),
-            pltpu.VMEM((LAYERS, HID, DIM), jnp.bfloat16),
             pltpu.VMEM((DIM, SUB), jnp.float32),
             pltpu.VMEM((2, DIM, CHUNK), jnp.bfloat16),
             pltpu.SemaphoreType.DMA,
             pltpu.SemaphoreType.DMA((2,)),
             pltpu.SemaphoreType.DMA((LAYERS,)),
             pltpu.SemaphoreType.DMA((LAYERS, CHUNKS)),
+            pltpu.SemaphoreType.DMA((LAYERS, 3)),
+            pltpu.SemaphoreType.DMA((LAYERS, 3, CHUNKS)),
             pltpu.SemaphoreType.DMA((LAYERS, len(HALOS))),
             pltpu.SemaphoreType.DMA((LAYERS, len(HALOS))),
             pltpu.SemaphoreType.DMA((2,)),
@@ -230,7 +321,7 @@
         compiler_params=pltpu.CompilerParams(
             collective_id=0, has_side_effects=True, vmem_limit_bytes=60 * 1024 * 1024
         ),
-    )(stream_in, norm_gains, w_inner, w_outer)
+    )(stream_in, norm_gains, w_inner, jnp.swapaxes(w_outer, 1, 2))
 
 
 def solution(mesh):

time: 126 us -> 79.7 us (0.63)
  the two profiles are of different devices: /device:TPU:2 before, /device:TPU:34 now
where the time goes in v1:
time: 79.7 us; the launch traced here: 79.6 us
  Pallas kernels  74.1 us (93%)
  local copies, waits for them, and re-layouts  5.43 us (7%)
    pallas_call x1, Pallas kernels, per_device(): pl.pallas_call(body, out_shape=jax.ShapeDtypeStruct(stream_in.shape, stre...  74.1 us
    unnamed x1, local copies, waits for them, and re-layouts  5.43 us

profile of v1, /device:TPU:34, one launch (start us, length us, event | category | flops | bytes accessed | tf_op | source)
XLA Modules:
  0.0 79.6 jit_solution(8639408485196284489)
XLA Ops:
  0.0 74.1 %shard_map.46 = bf16[320,8192]{1,0:T(8,128)(2,1)} custom-call(bf16[320,8192]{1,0:T(8,128)(2,1)} %x_ref.1, f32[2,320]{1,0:T(2,128)} %gain_ref.1, bf16[2,320,640]{2,1,0:T(8,128)(2,1)} %inner_ref.1, bf16[2,320,640]{2,1,0:T(8,128)(2,1)} %bitcast.1), custom_call_target="tpu_custom_call" | custom-call | tf_op jit(solution)/shard_map/pallas_call | solution.py:295
  74.1 5.4 %copy.6 = bf16[320,8192]{1,0:T(8,128)(2,1)} copy(bf16[320,8192]{1,0:T(8,128)(2,1)} %shard_map.46) | data formatting | bytes 10485760

commit v2 on v1

--- a/solution.py
+++ b/solution.py
@@ -25,17 +25,24 @@
 FAR = tuple(2**e for e in range(TRACKS - NEAR))
 HOP2, HOP8, HOP16 = range(3)
 HOP_TRACK = (1, 3, 4)
-LEAD = 2
-
-HALOS = (
-    (0, 128, 128, 7),
-    (128, 16, 256, 7),
-    (144, 16, 512, 7),
-    (192, 16, 1024, 4),
-    (192, 16, 1024, 5),
-    (176, 32, 1024, 6),
-    (160, 48, 1024, 7),
-)
+WINDOW = 5
+LEAD = 3
+LAG = 4
+
+
+def tails():
+    pieces = [(0, 8 * WIDTH, LANES, CHUNKS - 1)]
+    for track in range(8, NEAR):
+        if 2**track < CHUNK:
+            pieces.append((track * WIDTH, WIDTH, 2**track, CHUNKS - 1))
+    for chunk in range(CHUNKS):
+        need = [track for track in range(NEAR) if CHUNK <= 2**track and COLS - 2**track <= chunk * CHUNK]
+        if need:
+            pieces.append((need[0] * WIDTH, NEAR_ROWS - need[0] * WIDTH, CHUNK, chunk))
+    return tuple(pieces)
+
+
+HALOS = tails()
 
 
 def halo_slices(index):
@@ -46,8 +53,8 @@
 
 def body(
     x_ref, gain_ref, inner_ref, outer_ref, out_ref,
-    near, far, made, hop, gains, inner_t, inner_raw, outer_t, rotated, staged,
-    local_sem, weight_sem, far_send, far_recv, hop_send, hop_recv, halo_send, halo_recv, out_sem,
+    near, far, made, hop, gains, inner_t, inner_raw, outer_t, rotated,
+    local_sem, weight_sem, far_send, far_recv, hop_send, hop_recv, halo_send, halo_recv,
 ):
     me = lax.axis_index("seq")
     row, depth = me // 32, lax.rem(me // 4, 8)
@@ -159,9 +166,12 @@
     for index in range(len(HALOS)):
         halo_copy(0, index, x_ref).start()
 
-    @pl.loop(0, CHUNKS)
+    def turn(step):
+        return lax.rem(step + CHUNKS // 2, CHUNKS)
+
+    @pl.loop(0, WINDOW)
     def _(step):
-        send_far(0, lax.rem(step + CHUNKS // 2, CHUNKS), x_ref, NEAR_ROWS)
+        send_far(0, turn(step), x_ref, NEAR_ROWS)
 
     for layer in range(LAYERS):
         gains[layer] = jnp.broadcast_to(gain_ref[layer : layer + 1, :], (LANES, DIM)).T
@@ -204,9 +214,6 @@
         for index in range(len(HALOS)):
             halo_copy(layer, index, source).wait_recv()
 
-    def turn(step):
-        return lax.rem(step + CHUNKS // 2, CHUNKS)
-
     for step in range(LEAD):
         forward(0, turn(step))
 
@@ -214,13 +221,17 @@
     def _(step):
         chunk = turn(step)
 
+        @pl.when(step < CHUNKS - WINDOW)
+        def _():
+            send_far(0, turn(step + WINDOW), x_ref, NEAR_ROWS)
+
         @pl.when(step < CHUNKS - LEAD)
         def _():
             forward(0, turn(step + LEAD))
 
-        @pl.when(step >= CHUNKS // 2)
-        def _():
-            forward(1, turn(step - CHUNKS // 2))
+        @pl.when(step >= LAG)
+        def _():
+            forward(1, turn(step - LAG))
 
         wait_far(0, chunk)
 
@@ -244,42 +255,29 @@
             def _():
                 halo_copy(1, index, near.at[1]).start()
 
-    def out_copy(slot, chunk):
-        cols = pl.ds(pl.multiple_of(chunk * CHUNK, CHUNK), CHUNK)
-        return pltpu.make_async_copy(staged.at[slot], out_ref.at[:, cols], out_sem.at[slot])
-
     @pl.loop(0, CHUNKS)
     def _(step):
         chunk = lax.rem(step + CHUNKS // 2, CHUNKS)
-        slot = lax.rem(step, 2)
-
-        @pl.when(step < CHUNKS // 2)
-        def _():
-            forward(1, turn(step + CHUNKS // 2))
+
+        @pl.when(step < LAG)
+        def _():
+            forward(1, turn(step + CHUNKS - LAG))
 
         wait_far(1, chunk)
 
         @pl.when(step == CHUNKS // 2)
         def _():
             wait_halos(1, near.at[1])
-
-        @pl.when(step >= 2)
-        def _():
-            out_copy(slot, chunk).wait()
 
         @pl.loop(0, CHUNK // SUB)
         def _(part):
             at = pl.multiple_of(chunk * CHUNK + part * SUB, SUB)
 
             def store(result):
-                staged[slot, :, pl.ds(pl.multiple_of(part * SUB, SUB), SUB)] = result
+                out_ref[:, pl.ds(at, SUB)] = result
 
             mix(1, at, store)
 
-        out_copy(slot, chunk).start()
-
-    out_copy(0, 0).wait()
-    out_copy(1, 0).wait()
     for layer in range(LAYERS):
         source = x_ref if layer == 0 else near.at[1]
         for index in range(len(HALOS)):
@@ -291,12 +289,13 @@
 
 
 def per_device(stream_in, norm_gains, w_inner, w_outer):
-    hbm = pl.BlockSpec(memory_space=pl.ANY)
+    hbm = pl.BlockSpec(memory_space=pltpu.HBM)
+    vmem = pl.BlockSpec(memory_space=pltpu.VMEM)
     return pl.pallas_call(
         body,
-        out_shape=jax.ShapeDtypeStruct(stream_in.shape, stream_in.dtype),
-        in_specs=[hbm, pl.BlockSpec(memory_space=pltpu.VMEM), hbm, hbm],
-        out_specs=hbm,
+        out_shape=pltpu.VMEM(stream_in.shape, stream_in.dtype),
+        in_specs=[hbm, vmem, hbm, hbm],
+        out_specs=vmem,
         scratch_shapes=[
             pltpu.VMEM((LAYERS, NEAR_ROWS, PAD + COLS), jnp.bfloat16),
             pltpu.VMEM((LAYERS, FAR_ROWS, COLS), jnp.bfloat16),
@@ -307,7 +306,6 @@
             pltpu.VMEM((LAYERS, DIM, HID), jnp.bfloat16),
             pltpu.VMEM((LAYERS, DIM, HID), jnp.bfloat16),
             pltpu.VMEM((DIM, SUB), jnp.float32),
-            pltpu.VMEM((2, DIM, CHUNK), jnp.bfloat16),
             pltpu.SemaphoreType.DMA,
             pltpu.SemaphoreType.DMA((2,)),
             pltpu.SemaphoreType.DMA((LAYERS,)),
@@ -316,10 +314,9 @@
             pltpu.SemaphoreType.DMA((LAYERS, 3, CHUNKS)),
             pltpu.SemaphoreType.DMA((LAYERS, len(HALOS))),
             pltpu.SemaphoreType.DMA((LAYERS, len(HALOS))),
-            pltpu.SemaphoreType.DMA((2,)),
         ],
         compiler_params=pltpu.CompilerParams(
-            collective_id=0, has_side_effects=True, vmem_limit_bytes=60 * 1024 * 1024
+            collective_id=0, has_side_effects=True, vmem_limit_bytes=61_600_000
         ),
     )(stream_in, norm_gains, w_inner, jnp.swapaxes(w_outer, 1, 2))
 

time: 79.7 us -> 70.4 us (0.88)
  the two profiles are of different devices: /device:TPU:34 before, /device:TPU:2 now
where the time goes in v2:
time: 70.4 us; the launch traced here: 70.3 us
  Pallas kernels  67.9 us (96%)
  local copies, waits for them, and re-layouts  2.36 us (3%)
    pallas_call x1, Pallas kernels, per_device(): pl.pallas_call(body, out_shape=pltpu.VMEM(stream_in.shape, stream_in.dtyp...  67.9 us
    unnamed x1, local copies, waits for them, and re-layouts  2.36 us

profile of v2, /device:TPU:2, one launch (start us, length us, event | category | flops | bytes accessed | tf_op | source)
XLA Modules:
  0.0 70.3 jit_solution(8033883328836530317)
XLA Ops:
  0.0 67.9 %shard_map.46 = bf16[320,8192]{1,0:T(8,128)(2,1)S(1)} custom-call(bf16[320,8192]{1,0:T(8,128)(2,1)} %x_ref.1, f32[2,320]{1,0:T(2,128)} %gain_ref.1, bf16[2,320,640]{2,1,0:T(8,128)(2,1)} %inner_ref.1, bf16[2,320,640]{2,1,0:T(8,128)(2,1)} %bitcast.1), custom_call_target="tpu_custom_call" | custom-call | tf_op jit(solution)/shard_map/pallas_call | solution.py:294
  67.9 2.4 %copy.6 = bf16[320,8192]{1,0:T(8,128)(2,1)} copy(bf16[320,8192]{1,0:T(8,128)(2,1)S(1)} %shard_map.46) | data formatting | bytes 10485760

commit v3 on v2

--- a/solution.py
+++ b/solution.py
@@ -20,8 +20,10 @@
 PAD = 4096
 CHUNKS = 8
 CHUNK = COLS // CHUNKS
-SUB = 512
+SUB = 1024
 LANES = 128
+LAST = CHUNKS // 2 - 1
+VMEM_BODY = 57_000_000
 FAR = tuple(2**e for e in range(TRACKS - NEAR))
 HOP2, HOP8, HOP16 = range(3)
 HOP_TRACK = (1, 3, 4)
@@ -51,9 +53,23 @@
     return pl.ds(row, rows), start, cols
 
 
+def blend(rotated, gain, inner_t, outer_t):
+    values = rotated[...]
+    average = jnp.sum(values, axis=0, keepdims=True) * (1.0 / DIM)
+    centred = values - average
+    spread = jnp.sum(centred * centred, axis=0, keepdims=True) * (1.0 / DIM)
+    scale = lax.rsqrt(spread + 1e-05)
+    gain = jnp.concatenate([gain] * (SUB // LANES), axis=1)
+    normed = (centred * scale * gain).astype(jnp.bfloat16)
+    inner_sum = jnp.dot(inner_t, normed, preferred_element_type=jnp.float32)
+    hidden = (0.5 * inner_sum * (1.0 + lax.erf(inner_sum * (0.5**0.5)))).astype(jnp.bfloat16)
+    outer_sum = jnp.dot(outer_t, hidden, preferred_element_type=jnp.float32)
+    return (rotated[...] + outer_sum).astype(jnp.bfloat16)
+
+
 def body(
-    x_ref, gain_ref, inner_ref, outer_ref, out_ref,
-    near, far, made, hop, gains, inner_t, inner_raw, outer_t, rotated,
+    x_ref, gain_ref, inner_ref, outer_ref, out_ref, rest_ref, gains, inner_t, outer_t,
+    near, far, made, hop, inner_raw, rotated,
     local_sem, weight_sem, far_send, far_recv, hop_send, hop_recv, halo_send, halo_recv,
 ):
     me = lax.axis_index("seq")
@@ -181,7 +197,7 @@
     outer_copy.wait()
     near_copy.wait()
 
-    def mix(layer, at, store):
+    def gather_near(layer, at, keep):
         base = pl.multiple_of(PAD + at, LANES)
         for track in range(NEAR):
             shift = 2**track
@@ -191,19 +207,15 @@
                 piece = pltpu.roll(wide.astype(jnp.float32), shift, 1)[:, LANES:]
             else:
                 piece = near[layer, rows, pl.ds(pl.multiple_of(base - shift, LANES), SUB)].astype(jnp.float32)
+            keep(rows, piece)
+
+    def mix(layer, at, store):
+        def keep(rows, piece):
             rotated[rows, :] = piece
+
+        gather_near(layer, at, keep)
         rotated[NEAR_ROWS:, :] = far[layer, :, pl.ds(pl.multiple_of(at, LANES), SUB)].astype(jnp.float32)
-        values = rotated[...]
-        average = jnp.sum(values, axis=0, keepdims=True) * (1.0 / DIM)
-        centred = values - average
-        spread = jnp.sum(centred * centred, axis=0, keepdims=True) * (1.0 / DIM)
-        scale = lax.rsqrt(spread + 1e-05)
-        gain = jnp.concatenate([gains[layer]] * (SUB // LANES), axis=1)
-        normed = (centred * scale * gain).astype(jnp.bfloat16)
-        inner_sum = jnp.dot(inner_t[layer], normed, preferred_element_type=jnp.float32)
-        hidden = (0.5 * inner_sum * (1.0 + lax.erf(inner_sum * (0.5**0.5)))).astype(jnp.bfloat16)
-        outer_sum = jnp.dot(outer_t[layer], hidden, preferred_element_type=jnp.float32)
-        store((rotated[...] + outer_sum).astype(jnp.bfloat16))
+        store(blend(rotated, gains[layer], inner_t[layer], outer_t[layer]))
 
     def wait_far(layer, chunk):
         cols = pl.ds(pl.multiple_of(chunk * CHUNK, CHUNK), CHUNK)
@@ -255,7 +267,7 @@
             def _():
                 halo_copy(1, index, near.at[1]).start()
 
-    @pl.loop(0, CHUNKS)
+    @pl.loop(0, CHUNKS - 1)
     def _(step):
         chunk = lax.rem(step + CHUNKS // 2, CHUNKS)
 
@@ -278,6 +290,16 @@
 
             mix(1, at, store)
 
+    for part in range(CHUNK // SUB):
+        cols = pl.ds(part * SUB, SUB)
+
+        def keep(rows, piece):
+            rest_ref[rows, cols] = piece.astype(jnp.bfloat16)
+
+        gather_near(1, LAST * CHUNK + part * SUB, keep)
+
+    wait_far(1, LAST)
+    rest_ref[NEAR_ROWS:, :] = far[1, :, pl.ds(LAST * CHUNK, CHUNK)]
     for layer in range(LAYERS):
         source = x_ref if layer == 0 else near.at[1]
         for index in range(len(HALOS)):
@@ -288,22 +310,43 @@
             where(passes[kind], lambda: pltpu.make_async_copy(kept, kept, hop_send.at[layer, kind]).wait())
 
 
+def finish(part_ref, rest_ref, gains, inner_t, outer_t, out_ref, rotated, made, sem):
+    def copy(chunk, source, start):
+        cols = pl.ds(chunk * CHUNK, CHUNK)
+        return pltpu.make_async_copy(source.at[:, pl.ds(start, CHUNK)], out_ref.at[:, cols], sem.at[chunk])
+
+    copies = [copy(chunk, part_ref, chunk * CHUNK) for chunk in range(CHUNKS) if chunk != LAST]
+    for each in copies:
+        each.start()
+    for part in range(CHUNK // SUB):
+        cols = pl.ds(part * SUB, SUB)
+        rotated[...] = rest_ref[:, cols].astype(jnp.float32)
+        made[:, cols] = blend(rotated, gains[1], inner_t[1], outer_t[1])
+    copies.append(copy(LAST, made, 0))
+    copies[-1].start()
+    for each in copies:
+        each.wait()
+
+
 def per_device(stream_in, norm_gains, w_inner, w_outer):
     hbm = pl.BlockSpec(memory_space=pltpu.HBM)
     vmem = pl.BlockSpec(memory_space=pltpu.VMEM)
-    return pl.pallas_call(
+    kept = pl.pallas_call(
         body,
-        out_shape=pltpu.VMEM(stream_in.shape, stream_in.dtype),
+        out_shape=[
+            pltpu.VMEM((DIM, COLS), jnp.bfloat16),
+            pltpu.VMEM((DIM, CHUNK), jnp.bfloat16),
+            pltpu.VMEM((LAYERS, DIM, LANES), jnp.float32),
+            pltpu.VMEM((LAYERS, HID, DIM), jnp.bfloat16),
+            pltpu.VMEM((LAYERS, DIM, HID), jnp.bfloat16),
+        ],
         in_specs=[hbm, vmem, hbm, hbm],
-        out_specs=vmem,
+        out_specs=[vmem] * 5,
         scratch_shapes=[
             pltpu.VMEM((LAYERS, NEAR_ROWS, PAD + COLS), jnp.bfloat16),
             pltpu.VMEM((LAYERS, FAR_ROWS, COLS), jnp.bfloat16),
             pltpu.VMEM((FAR_ROWS, COLS), jnp.bfloat16),
             pltpu.VMEM((LAYERS, 3, WIDTH, COLS), jnp.bfloat16),
-            pltpu.VMEM((LAYERS, DIM, LANES), jnp.float32),
-            pltpu.VMEM((LAYERS, HID, DIM), jnp.bfloat16),
-            pltpu.VMEM((LAYERS, DIM, HID), jnp.bfloat16),
             pltpu.VMEM((LAYERS, DIM, HID), jnp.bfloat16),
             pltpu.VMEM((DIM, SUB), jnp.float32),
             pltpu.SemaphoreType.DMA,
@@ -316,9 +359,23 @@
             pltpu.SemaphoreType.DMA((LAYERS, len(HALOS))),
         ],
         compiler_params=pltpu.CompilerParams(
-            collective_id=0, has_side_effects=True, vmem_limit_bytes=61_600_000
+            collective_id=0, has_side_effects=True, vmem_limit_bytes=VMEM_BODY
         ),
+        name="mix_and_send",
     )(stream_in, norm_gains, w_inner, jnp.swapaxes(w_outer, 1, 2))
+    return pl.pallas_call(
+        finish,
+        out_shape=jax.ShapeDtypeStruct(stream_in.shape, stream_in.dtype),
+        in_specs=[vmem] * 5,
+        out_specs=hbm,
+        scratch_shapes=[
+            pltpu.VMEM((DIM, SUB), jnp.float32),
+            pltpu.VMEM((DIM, CHUNK), jnp.bfloat16),
+            pltpu.SemaphoreType.DMA((CHUNKS,)),
+        ],
+        compiler_params=pltpu.CompilerParams(vmem_limit_bytes=32 * 1024 * 1024),
+        name="last_chunk_and_store",
+    )(*kept)
 
 
 def solution(mesh):

time: 70.4 us -> 67.4 us (0.957); the launches traced: 70.3 us -> 66.3 us
  local copies, waits for them, and re-layouts: 2.36 us -> 0 us
  Pallas kernels: 67.9 us -> 66.3 us
    unnamed x1 -> x0, local copies, waits for them, and re-layouts: 2.36 us -> none
    pallas_call x1 -> x2, Pallas kernels: 67.9 us -> 66.3 us  [the longest x1 63.3 us: per_device(): pl.pallas_call(body, out_shape=[pltpu.VMEM((DIM, COLS), jnp.bfloat16), pl...]
where the time goes in v3:
time: 67.4 us; the launch traced here: 66.3 us
  Pallas kernels  66.3 us (98%)
    pallas_call x1, Pallas kernels, per_device(): pl.pallas_call(body, out_shape=[pltpu.VMEM((DIM, COLS), jnp.bfloat16), pl...  63.3 us
    pallas_call x1, Pallas kernels, per_device(): pl.pallas_call(finish, out_shape=jax.ShapeDtypeStruct(stream_in.shape, st...  3.01 us

profile of v3, /device:TPU:2, one launch (start us, length us, event | category | flops | bytes accessed | tf_op | source)
XLA Modules:
  0.0 66.3 jit_solution(1318998431277333414)
XLA Ops:
  0.0 63.3 %mix_and_send.1 = (bf16[320,8192]{1,0:T(8,128)(2,1)S(1)}, bf16[320,1024]{1,0:T(8,128)(2,1)S(1)}, f32[2,320,128]{2,1,0:T(8,128)S(1)}, bf16[2,640,320]{2,1,0:T(8,128)(2,1)S(1)}, bf16[2,320,640]{2,1,0:T(8,128)(2,1)S(1)}) custom-call(bf16[320,8192]{1,0:T(8,128)(2,1)} %x_ref.1, f32[2,320]{1,0:T(2,128)} %gain_ref.1, bf16[2,320,640]{2,1,0:T(8,128)(2,1)} %inner_ref.1, ...), custom_call_target="tpu_custom_call" | custom-call | tf_op jit(solution)/shard_map/mix_and_send/pallas_call | solution.py:334
  63.3 3.0 %last_chunk_and_store.1 = bf16[320,8192]{1,0:T(8,128)(2,1)} custom-call(bf16[320,8192]{1,0:T(8,128)(2,1)S(1)} %get-tuple-element.10.part_ref, bf16[320,1024]{1,0:T(8,128)(2,1)S(1)} %get-tuple-element.11.rest_ref, f32[2,320,128]{2,1,0:T(8,128)S(1)} %get-tuple-element.12.gains, bf16[2,640,320]{2,1,0:T(8,128)(2,1)S(1)} %get-tuple-element.13.inner_t, ...), custom_call_target="tpu_custom_call" | custom-call | tf_op jit(solution)/shard_map/last_chunk_and_store/pallas_call | solution.py:366

commit v4 on v3

--- a/solution.py
+++ b/solution.py
@@ -27,8 +27,8 @@
 FAR = tuple(2**e for e in range(TRACKS - NEAR))
 HOP2, HOP8, HOP16 = range(3)
 HOP_TRACK = (1, 3, 4)
-WINDOW = 5
-LEAD = 3
+WINDOW = 6
+LEAD = 4
 LAG = 4
 
 
@@ -114,7 +114,9 @@
     outer_copy.start()
 
     barrier = pltpu.get_barrier_semaphore()
-    peers = ahead + behind + hop_to + hop_from + pass_to + pass_from
+    direct = [track for track in range(len(FAR)) if track != HOP_TRACK[HOP16]]
+    peers = [ahead[track] for track in direct] + [behind[track] for track in direct]
+    peers += hop_to + hop_from + pass_to + pass_from
     for peer in peers:
         pl.semaphore_signal(barrier, inc=1, device_id={"seq": peer})
     pl.semaphore_wait(barrier, len(peers))
@@ -179,13 +181,17 @@
 
             where(passes[kind], relay)
 
+    def turn(step):
+        return lax.rem(step + CHUNKS // 2, CHUNKS)
+
+    @pl.loop(0, 2)
+    def _(step):
+        send_far(0, turn(step), x_ref, NEAR_ROWS)
+
     for index in range(len(HALOS)):
         halo_copy(0, index, x_ref).start()
 
-    def turn(step):
-        return lax.rem(step + CHUNKS // 2, CHUNKS)
-
-    @pl.loop(0, WINDOW)
+    @pl.loop(2, WINDOW)
     def _(step):
         send_far(0, turn(step), x_ref, NEAR_ROWS)
 

time: 67.4 us -> 65.3 us (0.969)
  Pallas kernels: 66.3 us -> 64.1 us
    pallas_call x1, Pallas kernels: 63.3 us -> 61.1 us  [per_device(): pl.pallas_call(body, out_shape=[pltpu.VMEM((DIM, COLS), jnp.bfloat16), pl...]
where the time goes in v4:
time: 65.3 us; the launch traced here: 64.1 us
  Pallas kernels  64.1 us (98%)
    pallas_call x1, Pallas kernels, per_device(): pl.pallas_call(body, out_shape=[pltpu.VMEM((DIM, COLS), jnp.bfloat16), pl...  61.1 us
    pallas_call x1, Pallas kernels, per_device(): pl.pallas_call(finish, out_shape=jax.ShapeDtypeStruct(stream_in.shape, st...  3.01 us

profile of v4, /device:TPU:2, one launch (start us, length us, event | category | flops | bytes accessed | tf_op | source)
XLA Modules:
  0.0 64.1 jit_solution(8942292107200503122)
XLA Ops:
  0.0 61.1 %mix_and_send.1 = (bf16[320,8192]{1,0:T(8,128)(2,1)S(1)}, bf16[320,1024]{1,0:T(8,128)(2,1)S(1)}, f32[2,320,128]{2,1,0:T(8,128)S(1)}, bf16[2,640,320]{2,1,0:T(8,128)(2,1)S(1)}, bf16[2,320,640]{2,1,0:T(8,128)(2,1)S(1)}) custom-call(bf16[320,8192]{1,0:T(8,128)(2,1)} %x_ref.1, f32[2,320]{1,0:T(2,128)} %gain_ref.1, bf16[2,320,640]{2,1,0:T(8,128)(2,1)} %inner_ref.1, ...), custom_call_target="tpu_custom_call" | custom-call | tf_op jit(solution)/shard_map/mix_and_send/pallas_call | solution.py:340
  61.1 3.0 %last_chunk_and_store.1 = bf16[320,8192]{1,0:T(8,128)(2,1)} custom-call(bf16[320,8192]{1,0:T(8,128)(2,1)S(1)} %get-tuple-element.10.part_ref, bf16[320,1024]{1,0:T(8,128)(2,1)S(1)} %get-tuple-element.11.rest_ref, f32[2,320,128]{2,1,0:T(8,128)S(1)} %get-tuple-element.12.gains, bf16[2,640,320]{2,1,0:T(8,128)(2,1)S(1)} %get-tuple-element.13.inner_t, ...), custom_call_target="tpu_custom_call" | custom-call | tf_op jit(solution)/shard_map/last_chunk_and_store/pallas_call | solution.py:372
